TPU v7x, 128 devices: a whole 4x4x4 slice. The times are simulated.
128 devices in a mesh: row: 8 (over y, core), col: 16 (over z, x).
Axes of the slice: x: 4, y: 4, z: 4, core: 2. Of those that a mesh axis runs over, the one named last changes fastest.
Arguments:
- raster: float32 [256, 2048, 128], P('row', 'col'), may hold values from -6 to 6
- slot_of: int32 [256, 2048], P('row', 'col'), may hold values from 0 to 4095, as said below
- slot_target: int32 [8, 16, 4096], P('row', 'col'), may hold values from 0 to 1024, as said below
Outputs:
- parcel_means: float32 [131072, 128], P(('row', 'col'))
- anomaly: float32 [256, 2048, 128], P('row', 'col')
Inputs may be any that keep to these rules, and one draw needn't show every extreme that they name: `slot_of`: A pixel's slot s is a used slot of its tile: slot_target of that tile at s is below 1024. Slot s belongs to the owner of index s // 32, numbered i * 16 + j. `slot_target`: 1024 marks an empty slot. Within one tile and one owner the used slots come first and name distinct rows; one tile may use from 1 to 32 slots of one owner; every tile fills its own block of 32 and one owner gets a full block from every tile.
All inputs are finite; a program needn't handle non-finite values.
Results may differ from a plain program's by a relative error of at most 0.00007.
Values sent between devices are 32-bit elements; how exact they have to be, the bound alone decides.
A program may use at most 64 MiB of HBM per device.

v0:
```python
import itertools

import jax
import jax.numpy as jnp
from jax import lax
from jax.experimental import pallas as pl
from jax.experimental.pallas import tpu as pltpu
from jax.sharding import PartitionSpec as P

MESH = pl.DeviceIdType.MESH
PIX = 4096
BANDS = 128
PAR_DEV = 1024
CAP = 32
DEVS = 128
BLK = 8
ROWS = BLK * CAP
BATCHES = DEVS // BLK
EARLY = 2
BF = jnp.bfloat16
F32 = jnp.float32
I16 = jnp.int16


def _hops(d):
    return sum(min(v, 4 - v) for v in d)


ORDER = sorted(itertools.product(range(4), repeat=3), key=lambda d: (-_hops(d),) + d)
CODES = [d[0] + 4 * d[1] + 16 * d[2] for d in ORDER]


def pick(values, index):
    got = jnp.int32(values[0])
    for n, v in enumerate(values[1:], 1):
        got = jnp.where(index == n, jnp.int32(v), got)
    return got


def split(v):
    hi = v.astype(BF)
    lo = (v - hi.astype(F32)).astype(BF)
    return hi, lo


def onehot(mask):
    return jnp.where(mask, jnp.ones((), BF), jnp.zeros((), BF))


def kernel(
    raster, slots, targets, tot, acc,
    x2, oh, b1, rowb, colb, tcol, inv, m2,
    send, got, rep, ret, small_out, small_in, slot_v, targ_v,
    s_in, s_send, s_got, s_small, s_ret,
):
    row, col = lax.axis_index("row"), lax.axis_index("col")
    x, y, z, core = col % 4, row // 2, col // 4, row % 2
    me = row * 16 + col

    def place(code, sign):
        dx, dy, dz = code % 4, (code // 4) % 4, code // 16
        return (x + sign * dx + 4) % 4, (y + sign * dy + 4) % 4, (z + sign * dz + 4) % 4

    def lin(tx, ty, tz, tc):
        return (ty * 2 + tc) * 16 + tz * 4 + tx

    def remote(src, dst, send_sem, recv_sem, t):
        tx, ty, tz, tc = t
        pltpu.make_async_remote_copy(
            src_ref=src, dst_ref=dst, send_sem=send_sem, recv_sem=recv_sem,
            device_id=(ty * 2 + tc, tz * 4 + tx), device_id_type=MESH,
        ).start()

    def send_or_keep(src, dst, send_sem, recv_sem, t, may_be_self):
        if not may_be_self:
            remote(src, dst, send_sem, recv_sem, t)
            return
        mine = lin(*t) == me

        @pl.when(jnp.logical_not(mine))
        def _():
            remote(src, dst, send_sem, recv_sem, t)

        @pl.when(mine)
        def _():
            pltpu.make_async_copy(src, dst, recv_sem).start()

    def wait_bytes(ref, sem):
        pltpu.make_async_copy(ref, ref, sem).wait()

    in_slots = pltpu.make_async_copy(slots, slot_v, s_in.at[0])
    in_targets = pltpu.make_async_copy(targets, targ_v, s_in.at[1])
    in_slots.start()
    in_targets.start()
    quarter = PIX // 4
    in_raster = []
    for n in range(4):
        part = pl.ds(n * quarter, quarter)
        in_raster.append(pltpu.make_async_copy(raster.at[part], acc.at[part], s_in.at[2 + n]))
        in_raster[-1].start()
    barrier = pltpu.get_barrier_semaphore()

    def greet(n, carry):
        t = (me + n) % DEVS
        pl.semaphore_signal(barrier, inc=1, device_id=(t // 16, t % 16), device_id_type=MESH)
        return carry

    lax.fori_loop(1, DEVS, greet, 0)

    in_slots.wait()
    for r in range(32):
        rowb[16 * r : 16 * r + 16, :] = jnp.broadcast_to(slot_v[r : r + 1, :], (16, 128)).astype(I16)
    for n in range(4):
        in_raster[n].wait()
        for h in range(4):
            a = n * quarter + h * 256
            hi, lo = split(acc[a : a + 256, :])
            x2[a : a + 256, 0:128] = hi
            x2[a : a + 256, 128:256] = lo

    iota32 = lax.broadcasted_iota(jnp.int32, (32, 128), 0)

    def sum_batch(b):
        g, bb = b // 8, b % 8
        places = [place(pick(CODES[k::8], bb), 1) + (g,) for k in range(BLK)]
        ids = jnp.concatenate([(iota32 + lin(*t) * CAP).astype(I16) for t in places], axis=0)
        ids = ids.reshape(16, 16, 128)
        for r in range(32):
            m = rowb[16 * r : 16 * r + 16, :][None] == ids
            oh[:, 128 * r : 128 * r + 128] = onehot(m).reshape(ROWS, 128)
        s = jnp.dot(oh[...], x2[...], preferred_element_type=F32)
        send[pl.ds(pl.multiple_of(b * ROWS, ROWS), ROWS), :] = s[:, :128] + s[:, 128:]

    def send_batch(b):
        g, bb = b // 8, b % 8
        for k in range(BLK):
            i = bb * 8 + k
            t = place(pick(CODES[k::8], bb), 1) + (g,)
            src = send.at[pl.ds(pl.multiple_of((b * 8 + k) * CAP, CAP), CAP)]
            dst = got.at[pl.ds(pl.multiple_of((i * 2 + core) * CAP, CAP), CAP)]
            send_or_keep(src, dst, s_send.at[0], s_got.at[bb * 2 + k // 4], t, k == 7)

    for b in range(EARLY):
        sum_batch(b)
    pl.semaphore_wait(barrier, DEVS - 1)
    for b in range(EARLY):
        send_batch(b)

    pad = jnp.zeros((96, 128), jnp.int32)
    turned = jnp.concatenate([slot_v[...], pad], axis=0).T
    lane16 = lax.broadcasted_iota(jnp.int32, (128, 128), 1).astype(I16)
    for r in range(32):
        c = jnp.broadcast_to(turned[:, r : r + 1], (128, 128))
        colb[128 * r : 128 * r + 128, :] = c.astype(I16)
        b1[128 * r : 128 * r + 128, :] = onehot((c % 128).astype(I16) == lane16)
        hi_row = jnp.broadcast_to(slot_v[r : r + 1, :] // 128, (32, 128)).astype(I16)
        oh[0:32, 128 * r : 128 * r + 128] = onehot(hi_row == iota32.astype(I16))
    counts = jnp.dot(oh[0:32, :], b1[...], preferred_element_type=F32)
    in_targets.wait()
    targ = targ_v[...].astype(F32)
    lane = lax.broadcasted_iota(jnp.int32, (32, 128), 1)
    for m in range(4):
        t = pltpu.roll(targ, (128 - 32 * m) % 128, 1)
        c = pltpu.roll(counts, (128 + 32 - 32 * m) % 128, 1)
        v = jnp.where(lane < 32, t, jnp.where(lane < 64, c, 0.0))
        small_out[pl.ds(m, 32, stride=4), :] = v

    def send_small(i, carry):
        code = pick(CODES, i)
        for g in range(2):
            t = place(code, 1) + (g,)
            src = small_out.at[pl.ds(lin(*t), 1)]
            dst = small_in.at[pl.ds(i * 2 + core, 1)]
            send_or_keep(src, dst, s_send.at[1], s_small.at[0], t, True)
        return carry

    lax.fori_loop(0, 64, send_small, 0)

    def batch(b, carry):
        sum_batch(b)
        send_batch(b)
        return carry

    lax.fori_loop(EARLY, BATCHES, batch, 0)

    wait_bytes(small_in, s_small.at[0])
    t_all = jnp.zeros((32, 128), F32)
    c_all = jnp.zeros((32, 128), F32)
    for m in range(4):
        v = small_in[pl.ds(m, 32, stride=4), :]
        group = lane // 32 == m
        t_all = jnp.where(group, pltpu.roll(v, (32 * m) % 128, 1), t_all)
        c_all = jnp.where(group, pltpu.roll(v, (128 + 32 * m - 32) % 128, 1), c_all)
    targ_v[...] = t_all.astype(jnp.int32)
    slot_v[...] = c_all.astype(jnp.int32)
    turned = jnp.concatenate([targ_v[...], pad], axis=0).T
    for r in range(32):
        rowb[16 * r : 16 * r + 16, :] = jnp.broadcast_to(targ_v[r : r + 1, :], (16, 128)).astype(I16)
        tcol[128 * r : 128 * r + 128, :] = jnp.broadcast_to(turned[:, r : r + 1], (128, 128)).astype(I16)

    iota64 = lax.broadcasted_iota(jnp.int32, (64, 128), 0)

    def number(n, carry):
        ids = iota64 + n * 64
        s = jnp.zeros((64, 128), F32)
        for r in range(32):
            m = jnp.broadcast_to(targ_v[r : r + 1, :], (64, 128)) == ids
            c = jnp.broadcast_to(slot_v[r : r + 1, :], (64, 128)).astype(F32)
            s = s + jnp.where(m, c, 0.0)
        s = jnp.sum(s, axis=1, keepdims=True)
        here = pl.ds(pl.multiple_of(n * 64, 64), 64)
        inv[here, :] = jnp.broadcast_to(1.0 / jnp.maximum(s, 1.0), (64, 128))
        tot[here, :] = jnp.zeros((64, 128), F32)
        return carry

    lax.fori_loop(0, PAR_DEV // 64, number, 0)

    iota256 = lax.broadcasted_iota(jnp.int32, (256, 128), 0)

    def gather_sums(b, carry):
        here = pl.ds(pl.multiple_of(b * ROWS, ROWS), ROWS)
        wait_bytes(got.at[here], s_got.at[b])
        r2 = jnp.concatenate(split(got[here, :]), axis=1)
        rows = [rowb[pl.ds(pl.multiple_of((2 * b + h) * 16, 16), 16), :][None] for h in range(2)]
        for n in range(4):
            ids = (iota256 + n * 256).astype(I16).reshape(16, 16, 128)
            table = jnp.concatenate([onehot(v == ids).reshape(256, 128) for v in rows], axis=1)
            s = jnp.dot(table, r2, preferred_element_type=F32)
            tot[n * 256 : n * 256 + 256, :] += s[:, :128] + s[:, 128:]
        return carry

    lax.fori_loop(0, BATCHES, gather_sums, 0)

    for n in range(4):
        part = slice(n * 256, n * 256 + 256)
        mean = tot[part, :] * inv[part, :]
        tot[part, :] = mean
        hi, lo = split(mean)
        m2[part, 0:128] = hi
        m2[part, 128:256] = lo

    lane256 = lax.broadcasted_iota(jnp.int32, (256, 128), 1)

    def reply(b, carry):
        here = pl.ds(pl.multiple_of(b * ROWS, ROWS), ROWS)
        wanted = tcol[here, :]
        table = jnp.concatenate(
            [onehot(wanted == (lane256 + 128 * n).astype(I16)) for n in range(8)], axis=1
        )
        s = jnp.dot(table, m2[...], preferred_element_type=F32)
        rep[here, :] = s[:, :128] + s[:, 128:]
        for k in range(4):
            i = b * 4 + k
            chip = place(pick(CODES[k::4], b), -1)
            for g in range(2):
                src = rep.at[pl.ds(pl.multiple_of((i * 2 + g) * CAP, CAP), CAP)]
                dst = ret.at[pl.ds(pl.multiple_of((core * 64 + i) * CAP, CAP), CAP)]
                send_or_keep(src, dst, s_send.at[2], s_ret.at[core * 8 + b // 2], chip + (g,), k == 3)
        return carry

    lax.fori_loop(0, BATCHES, reply, 0)

    lane16r = lax.broadcasted_iota(jnp.int32, (16, 128), 1)

    def subtract(n, r2, ids):
        part = pl.ds(pl.multiple_of(n * 256, 256), 256)
        px = colb[part, :].reshape(16, 16, 128)
        table = jnp.concatenate([onehot(px == v).reshape(256, 128) for v in ids], axis=1)
        s = jnp.dot(table, r2, preferred_element_type=F32)
        acc[part, :] = acc[part, :] - s[:, :128] - s[:, 128:]

    def read_batch(b, carry):
        here = pl.ds(pl.multiple_of(b * ROWS, ROWS), ROWS)
        g, bb = b // 8, b % 8
        ids = []
        for h in range(2):
            v = lane16r % 32
            for m in range(4):
                base = lin(*place(pick(CODES[4 * h + m :: 8], bb), 1), g) * CAP
                v = v + jnp.where(lane16r // 32 == m, base, 0)
            ids.append(v.astype(I16)[None])
        wait_bytes(ret.at[here], s_ret.at[b])
        r2 = jnp.concatenate(split(ret[here, :]), axis=1)
        for n in range(16):
            subtract(n, r2, ids)
        return carry

    lax.fori_loop(0, BATCHES, read_batch, 0)

    most = pl.ds(0, (DEVS - 1) * CAP)
    wait_bytes(send.at[most], s_send.at[0])
    wait_bytes(small_out.at[pl.ds(0, DEVS - 1)], s_send.at[1])
    wait_bytes(rep.at[most], s_send.at[2])


def per_device(raster, slot_of, slot_target):
    operands = (raster.reshape(PIX, BANDS), slot_of, slot_target.reshape(32, 128))
    here = pl.BlockSpec(memory_space=pltpu.VMEM)
    outside = pl.BlockSpec(memory_space=pltpu.HBM)
    table = pltpu.VMEM((PIX, BANDS), F32)
    means, anomaly = pl.pallas_call(
        kernel,
        out_shape=(
            jax.ShapeDtypeStruct((PAR_DEV, BANDS), F32),
            jax.ShapeDtypeStruct((PIX, BANDS), F32),
        ),
        in_specs=[outside] * 3,
        out_specs=(here, here),
        scratch_shapes=[
            pltpu.VMEM((PIX, 2 * BANDS), BF),
            pltpu.VMEM((ROWS, PIX), BF),
            pltpu.VMEM((PIX, 128), BF),
            pltpu.VMEM((512, 128), I16),
            pltpu.VMEM((PIX, 128), I16),
            pltpu.VMEM((PIX, 128), I16),
            pltpu.VMEM((PAR_DEV, BANDS), F32),
            pltpu.VMEM((PAR_DEV, 2 * BANDS), BF),
            table,
            table,
            table,
            table,
            pltpu.VMEM((DEVS, 128), F32),
            pltpu.VMEM((DEVS, 128), F32),
            pltpu.VMEM((32, 128), jnp.int32),
            pltpu.VMEM((32, 128), jnp.int32),
            pltpu.SemaphoreType.DMA((6,)),
            pltpu.SemaphoreType.DMA((3,)),
            pltpu.SemaphoreType.DMA((BATCHES,)),
            pltpu.SemaphoreType.DMA((1,)),
            pltpu.SemaphoreType.DMA((BATCHES,)),
        ],
        compiler_params=pltpu.CompilerParams(
            collective_id=0, has_side_effects=True, vmem_limit_bytes=48 * 2**20
        ),
    )(*(pltpu.with_memory_space_constraint(v, pltpu.HBM) for v in operands))
    return means, anomaly.reshape(raster.shape)


def solution(mesh):
    placed = (P("row", "col", None), P("row", "col"), P("row", "col", None))
    return jax.shard_map(
        per_device,
        mesh=mesh,
        in_specs=placed,
        out_specs=(P(("row", "col"), None), P("row", "col", None)),
        check_vma=False,
    )
```

profile of v0, /device:TPU:1, one launch (start us, length us, event | category | flops | bytes accessed | tf_op | source)
XLA Modules:
  0.0 81.3 jit_solution(16858363821008389638)
XLA Ops:
  0.6 78.5 %shard_map.50 = (f32[1024,128]{1,0:T(8,128)S(1)}, f32[4096,128]{1,0:T(8,128)S(1)}) custom-call(f32[4096,128]{1,0:T(8,128)} %bitcast.4, s32[32,128]{1,0:T(8,128)} %slots.1, s32[32,128]{1,0:T(8,128)} %bitcast.5), custom_call_target="tpu_custom_call" | custom-call | tf_op jit(solution)/shard_map/pallas_call | solution.py:301
  79.2 0.8 copy.7
  80.0 1.3 %copy.8 = f32[32,128,128]{2,1,0:T(8,128)} copy(f32[32,128,128]{2,1,0:T(8,128)S(1)} %bitcast.3) | data formatting | bytes 4194304
where the time goes:
time: 81.4 us; the launch traced here: 81.3 us
  Pallas kernels  78.5 us (96%)
  local copies, waits for them, and re-layouts  2.11 us (3%)
    pallas_call x1, Pallas kernels, per_device(): pl.pallas_call(kernel, out_shape=(jax.ShapeDtypeStruct((PAR_DEV, BANDS),...  78.5 us
    unnamed x2, local copies, waits for them, and re-layouts  2.11 us

commit v1 on v0

v1 whole, which is shorter than its diff:
```python
import itertools
import random

import jax
import jax.numpy as jnp
from jax import lax
from jax.experimental import pallas as pl
from jax.experimental.pallas import tpu as pltpu
from jax.sharding import PartitionSpec as P

MESH = pl.DeviceIdType.MESH
PIX = 4096
BANDS = 128
PAR_DEV = 1024
CAP = 32
MSG = CAP + 1
STEP = 40
DEVS = 128
BLK = 8
ROWS = BLK * CAP
BATCHES = DEVS // BLK
EARLY = 2
BF = jnp.bfloat16
F32 = jnp.float32
I16 = jnp.int16


ORDER = [d for d in itertools.product(range(4), repeat=3) if any(d)]
random.Random(0).shuffle(ORDER)
ORDER.append((0, 0, 0))
CODES = [d[0] + 4 * d[1] + 16 * d[2] for d in ORDER]


def pick(values, index):
    got = jnp.int32(values[0])
    for n, v in enumerate(values[1:], 1):
        got = jnp.where(index == n, jnp.int32(v), got)
    return got


def split(v):
    hi = v.astype(BF)
    lo = (v - hi.astype(F32)).astype(BF)
    return hi, lo


def onehot(mask):
    return jnp.where(mask, jnp.ones((), BF), jnp.zeros((), BF))


def over_rows(v):
    v = jnp.broadcast_to(v, (16, 128)).astype(I16)
    return jnp.concatenate([v] * 16, axis=0)


def kernel(
    raster, slots, targets, tot, acc,
    x2, b1, colb, tcol, num, m2,
    send, got, rep, ret, small, slot_v, targ_v,
    s_in, s_send, s_got, s_ret,
):
    row, col = lax.axis_index("row"), lax.axis_index("col")
    x, y, z, core = col % 4, row // 2, col // 4, row % 2
    me = row * 16 + col

    def place(code, sign):
        dx, dy, dz = lax.rem(code, 4), lax.rem(lax.div(code, 4), 4), lax.div(code, 16)
        return tuple(lax.rem(v + sign * d + 4, 4) for v, d in ((x, dx), (y, dy), (z, dz)))

    def lin(tx, ty, tz, tc):
        return (ty * 2 + tc) * 16 + tz * 4 + tx

    def remote(src, dst, send_sem, recv_sem, t):
        tx, ty, tz, tc = t
        pltpu.make_async_remote_copy(
            src_ref=src, dst_ref=dst, send_sem=send_sem, recv_sem=recv_sem,
            device_id=(ty * 2 + tc, tz * 4 + tx), device_id_type=MESH,
        ).start()

    def send_or_keep(src, dst, send_sem, recv_sem, t, may_be_self):
        if not may_be_self:
            remote(src, dst, send_sem, recv_sem, t)
            return
        mine = lin(*t) == me

        @pl.when(jnp.logical_not(mine))
        def _():
            remote(src, dst, send_sem, recv_sem, t)

        @pl.when(mine)
        def _():
            pltpu.make_async_copy(src, dst, recv_sem).start()

    def wait_bytes(ref, sem):
        pltpu.make_async_copy(ref, ref, sem).wait()

    in_slots = pltpu.make_async_copy(slots, slot_v, s_in.at[0])
    in_targets = pltpu.make_async_copy(targets, targ_v, s_in.at[1])
    in_slots.start()
    in_targets.start()
    quarter = PIX // 4
    in_raster = []
    for n in range(4):
        part = pl.ds(n * quarter, quarter)
        in_raster.append(pltpu.make_async_copy(raster.at[part], acc.at[part], s_in.at[2 + n]))
        in_raster[-1].start()
    barrier = pltpu.get_barrier_semaphore()

    def greet(n, carry):
        far = (row + n) % 8
        for k in range(16):
            there = (far, (col + k) % 16)
            pl.semaphore_signal(barrier, inc=1, device_id=there, device_id_type=MESH)
        return carry

    for k in range(1, 16):
        there = (row, (col + k) % 16)
        pl.semaphore_signal(barrier, inc=1, device_id=there, device_id_type=MESH)
    lax.fori_loop(1, 8, greet, 0)

    in_slots.wait()
    iota32 = lax.broadcasted_iota(jnp.int32, (32, 128), 0)

    pad = jnp.zeros((96, 128), jnp.int32)
    turned = jnp.concatenate([slot_v[...], pad], axis=0).T
    lane16 = lax.broadcasted_iota(jnp.int32, (128, 128), 1).astype(I16)
    table = []
    for r in range(32):
        c = jnp.broadcast_to(turned[:, r : r + 1], (128, 128))
        colb[128 * r : 128 * r + 128, :] = c
        b1[128 * r : 128 * r + 128, :] = onehot((c % 128).astype(I16) == lane16)
        high = jnp.broadcast_to(slot_v[r : r + 1, :] // 128, (32, 128)).astype(I16)
        table.append(onehot(high == iota32.astype(I16)))
    counts = jnp.dot(jnp.concatenate(table, axis=1), b1[...], preferred_element_type=F32)
    in_targets.wait()
    targ = targ_v[...].astype(F32)
    lane = lax.broadcasted_iota(jnp.int32, (32, 128), 1)
    for m in range(4):
        t = pltpu.roll(targ, (128 - 32 * m) % 128, 1)
        c = pltpu.roll(counts, (128 + 32 - 32 * m) % 128, 1)
        v = jnp.where(lane < 32, t, jnp.where(lane < 64, c, 0.0))
        small[pl.ds(m, 32, stride=4), :] = v

    for n in range(4):
        in_raster[n].wait()
        for h in range(4):
            a = n * quarter + h * 256
            hi, lo = split(acc[a : a + 256, :])
            x2[a : a + 256, 0:128] = hi
            x2[a : a + 256, 128:256] = lo

    def sum_batch(b):
        g, bb = lax.div(b, 8), lax.rem(b, 8)
        places = [place(pick(CODES[k::8], bb), 1) + (g,) for k in range(BLK)]
        ids = jnp.concatenate([(iota32 + lin(*t) * CAP).astype(I16) for t in places], axis=0)
        table = [onehot(over_rows(slot_v[r : r + 1, :]) == ids) for r in range(32)]
        s = jnp.dot(jnp.concatenate(table, axis=1), x2[...], preferred_element_type=F32)
        s = s[:, :128] + s[:, 128:]
        for k in range(BLK):
            at = (b * 8 + k) * STEP
            send[pl.ds(pl.multiple_of(at, 8), CAP), :] = s[k * CAP : k * CAP + CAP, :]
            send[pl.ds(at + CAP, 1), :] = small[pl.ds(lin(*places[k]), 1), :]

    def send_batch(b):
        g, bb = lax.div(b, 8), lax.rem(b, 8)
        for k in range(BLK):
            i = bb * 8 + k
            t = place(pick(CODES[k::8], bb), 1) + (g,)
            src = send.at[pl.ds(pl.multiple_of((b * 8 + k) * STEP, 8), MSG)]
            dst = got.at[pl.ds(pl.multiple_of((core * 64 + i) * STEP, 8), MSG)]
            send_or_keep(src, dst, s_send.at[0], s_got.at[core * 8 + bb], t, k == 7)

    def first(b, carry):
        sum_batch(b)
        return carry

    def then_send(b, carry):
        send_batch(b)
        return carry

    lax.fori_loop(0, EARLY, first, 0)
    pl.semaphore_wait(barrier, DEVS - 1)
    lax.fori_loop(0, EARLY, then_send, 0)

    def batch(b, carry):
        sum_batch(b)
        send_batch(b)
        return carry

    lax.fori_loop(EARLY, BATCHES, batch, 0)

    for n in range(4):
        part = slice(n * 256, n * 256 + 256)
        tot[part, :] = jnp.zeros((256, 128), F32)
        num[part, :] = jnp.zeros((256, 128), F32)
    iota256 = lax.broadcasted_iota(jnp.int32, (256, 128), 0)
    sub8 = lax.broadcasted_iota(jnp.int32, (8, 128), 0)
    lane8 = lax.broadcasted_iota(jnp.int32, (8, 128), 1)

    def in_lanes(v, first):
        w = jnp.zeros((8, 128), F32)
        for m in range(4):
            here = (lane8 // 32 == m) & (sub8 % 4 == m)
            w = jnp.where(here, pltpu.roll(v, (128 + 32 * m - first) % 128, 1), w)
        return [jnp.sum(w[4 * h : 4 * h + 4, :], axis=0, keepdims=True) for h in range(2)]

    def gather_sums(n, carry):
        b = (n % 2) * 8 + n // 2
        at = b * BLK * STEP
        wait_bytes(got.at[pl.ds(pl.multiple_of(at, 8), BLK * MSG)], s_got.at[b])
        block = [got[pl.ds(pl.multiple_of(at + k * STEP, 8), CAP), :] for k in range(BLK)]
        r2 = jnp.concatenate(split(jnp.concatenate(block, axis=0)), axis=1)
        extra = [got[pl.ds(at + k * STEP + CAP, 1), :] for k in range(BLK)]
        extra = jnp.concatenate(extra, axis=0)
        wanted = [v.astype(jnp.int32) for v in in_lanes(extra, 0)]
        counts = in_lanes(extra, CAP)
        turned = jnp.concatenate(wanted + [jnp.zeros((6, 128), jnp.int32)], axis=0).T
        for h in range(2):
            column = jnp.broadcast_to(turned[:, h : h + 1], (128, 128))
            tcol[pl.ds(pl.multiple_of(b * ROWS + h * 128, 128), 128), :] = column
        rows = [over_rows(v) for v in wanted]
        for n in range(4):
            part = slice(n * 256, n * 256 + 256)
            ids = iota256 + n * 256
            c = num[part, :]
            for h in range(2):
                c = c + jnp.where(wanted[h] == ids, counts[h], 0.0)
            num[part, :] = c
            table = jnp.concatenate([onehot(v == ids.astype(I16)) for v in rows], axis=1)
            s = jnp.dot(table, r2, preferred_element_type=F32)
            tot[part, :] += s[:, :128] + s[:, 128:]
        return carry

    lax.fori_loop(0, BATCHES, gather_sums, 0)

    for n in range(4):
        part = slice(n * 256, n * 256 + 256)
        number = jnp.sum(num[part, :], axis=1, keepdims=True)
        mean = tot[part, :] * (1.0 / jnp.maximum(number, 1.0))
        tot[part, :] = mean
        hi, lo = split(mean)
        m2[part, 0:128] = hi
        m2[part, 128:256] = lo

    lane256 = lax.broadcasted_iota(jnp.int32, (256, 128), 1)

    def reply(n, carry):
        g, bb = (core + n // 8) % 2, n % 8
        b = g * 8 + bb
        here = pl.ds(pl.multiple_of(b * ROWS, ROWS), ROWS)
        wanted = tcol[here, :].astype(I16)
        table = jnp.concatenate(
            [onehot(wanted == (lane256 + 128 * n).astype(I16)) for n in range(8)], axis=1
        )
        s = jnp.dot(table, m2[...], preferred_element_type=F32)
        rep[here, :] = s[:, :128] + s[:, 128:]
        for k in range(BLK):
            i = bb * 8 + k
            t = place(pick(CODES[k::8], bb), -1) + (g,)
            src = rep.at[pl.ds(pl.multiple_of((b * 8 + k) * CAP, CAP), CAP)]
            dst = ret.at[pl.ds(pl.multiple_of((core * 64 + i) * CAP, CAP), CAP)]
            send_or_keep(src, dst, s_send.at[1], s_ret.at[core * 8 + bb], t, k == 7)
        return carry

    lax.fori_loop(0, BATCHES, reply, 0)

    lane1 = lax.broadcasted_iota(jnp.int32, (1, 128), 1)

    def subtract(n, r2, ids):
        part = pl.ds(pl.multiple_of(n * 256, 256), 256)
        px = colb[part, :].astype(I16)
        table = jnp.concatenate([onehot(px == v) for v in ids], axis=1)
        s = jnp.dot(table, r2, preferred_element_type=F32)
        acc[part, :] = acc[part, :] - s[:, :128] - s[:, 128:]

    def read_batch(b, carry):
        here = pl.ds(pl.multiple_of(b * ROWS, ROWS), ROWS)
        g, bb = lax.div(b, 8), lax.rem(b, 8)
        ids = []
        for h in range(2):
            v = lane1 % 32
            for m in range(4):
                base = lin(*place(pick(CODES[4 * h + m :: 8], bb), 1), g) * CAP
                v = v + jnp.where(lane1 // 32 == m, base, 0)
            ids.append(over_rows(v))
        wait_bytes(ret.at[here], s_ret.at[b])
        r2 = jnp.concatenate(split(ret[here, :]), axis=1)
        for n in range(16):
            subtract(n, r2, ids)
        return carry

    lax.fori_loop(0, BATCHES, read_batch, 0)

    wait_bytes(send.at[pl.ds(0, (DEVS - 1) * MSG)], s_send.at[0])
    wait_bytes(rep.at[pl.ds(0, (DEVS - 1) * CAP)], s_send.at[1])


def per_device(raster, slot_of, slot_target):
    operands = (raster.reshape(PIX, BANDS), slot_of, slot_target.reshape(32, 128))
    here = pl.BlockSpec(memory_space=pltpu.VMEM)
    outside = pl.BlockSpec(memory_space=pltpu.HBM)
    table = pltpu.VMEM((PIX, BANDS), F32)
    means, anomaly = pl.pallas_call(
        kernel,
        out_shape=(
            jax.ShapeDtypeStruct((PAR_DEV, BANDS), F32),
            jax.ShapeDtypeStruct((PIX, BANDS), F32),
        ),
        in_specs=[outside] * 3,
        out_specs=(here, here),
        scratch_shapes=[
            pltpu.VMEM((PIX, 2 * BANDS), BF),
            pltpu.VMEM((PIX, 128), BF),
            pltpu.VMEM((PIX, 128), jnp.int32),
            pltpu.VMEM((PIX, 128), jnp.int32),
            pltpu.VMEM((PAR_DEV, BANDS), F32),
            pltpu.VMEM((PAR_DEV, 2 * BANDS), BF),
            pltpu.VMEM((DEVS * STEP, BANDS), F32),
            pltpu.VMEM((DEVS * STEP, BANDS), F32),
            table,
            table,
            pltpu.VMEM((DEVS, 128), F32),
            pltpu.VMEM((32, 128), jnp.int32),
            pltpu.VMEM((32, 128), jnp.int32),
            pltpu.SemaphoreType.DMA((6,)),
            pltpu.SemaphoreType.DMA((2,)),
            pltpu.SemaphoreType.DMA((BATCHES,)),
            pltpu.SemaphoreType.DMA((BATCHES,)),
        ],
        compiler_params=pltpu.CompilerParams(
            collective_id=0, has_side_effects=True, vmem_limit_bytes=48 * 2**20
        ),
    )(*(pltpu.with_memory_space_constraint(v, pltpu.HBM) for v in operands))
    return means, anomaly.reshape(raster.shape)


def solution(mesh):
    placed = (P("row", "col", None), P("row", "col"), P("row", "col", None))
    return jax.shard_map(
        per_device,
        mesh=mesh,
        in_specs=placed,
        out_specs=(P(("row", "col"), None), P("row", "col", None)),
        check_vma=False,
    )
```

time: 81.4 us -> 70.3 us (0.86); the launches traced: 81.3 us -> 68.9 us
  Pallas kernels: 78.5 us -> 66.2 us
    pallas_call x1, Pallas kernels: 78.5 us -> 66.2 us  [per_device(): pl.pallas_call(kernel, out_shape=(jax.ShapeDtypeStruct((PAR_DEV, BANDS),...]
where the time goes in v1:
time: 70.3 us; the launch traced here: 68.9 us
  Pallas kernels  66.2 us (94%)
  local copies, waits for them, and re-layouts  2.11 us (3%)
    pallas_call x1, Pallas kernels, per_device(): pl.pallas_call(kernel, out_shape=(jax.ShapeDtypeStruct((PAR_DEV, BANDS),...  66.2 us
    unnamed x2, local copies, waits for them, and re-layouts  2.11 us

profile of v1, /device:TPU:1, one launch (start us, length us, event | category | flops | bytes accessed | tf_op | source)
XLA Modules:
  0.0 68.9 jit_solution(2710318033314607211)
XLA Ops:
  0.6 66.2 %shard_map.50 = (f32[1024,128]{1,0:T(8,128)S(1)}, f32[4096,128]{1,0:T(8,128)S(1)}) custom-call(f32[4096,128]{1,0:T(8,128)} %bitcast.4, s32[32,128]{1,0:T(8,128)} %slots.1, s32[32,128]{1,0:T(8,128)} %bitcast.5), custom_call_target="tpu_custom_call" | custom-call | tf_op jit(solution)/shard_map/pallas_call | solution.py:303
  66.8 0.8 %copy.7 = f32[1024,128]{1,0:T(8,128)} copy(f32[1024,128]{1,0:T(8,128)S(1)} %get-tuple-element.8) | data formatting | bytes 1048576
  67.6 1.3 %copy.8 = f32[32,128,128]{2,1,0:T(8,128)} copy(f32[32,128,128]{2,1,0:T(8,128)S(1)} %bitcast.3) | data formatting | bytes 4194304

commit v2 on v1

--- a/solution.py
+++ b/solution.py
@@ -1,5 +1,4 @@
 import itertools
-import random
 
 import jax
 import jax.numpy as jnp
@@ -25,9 +24,8 @@
 I16 = jnp.int16
 
 
-ORDER = [d for d in itertools.product(range(4), repeat=3) if any(d)]
-random.Random(0).shuffle(ORDER)
-ORDER.append((0, 0, 0))
+SHIFTS = list(itertools.product(range(4), repeat=2))
+ORDER = [(t, (t + u) % 4, (t + v) % 4) for u, v in SHIFTS[1:] + SHIFTS[:1] for t in (2, 1, 3, 0)]
 CODES = [d[0] + 4 * d[1] + 16 * d[2] for d in ORDER]
 
 
@@ -106,17 +104,21 @@
         in_raster[-1].start()
     barrier = pltpu.get_barrier_semaphore()
 
+    around = [(k + 10) % 16 for k in range(16)]
+
     def greet(n, carry):
-        far = (row + n) % 8
-        for k in range(16):
-            there = (far, (col + k) % 16)
+        far = lax.rem(row + n, 8)
+        for k in around:
+            there = (far, lax.rem(col + k, 16))
             pl.semaphore_signal(barrier, inc=1, device_id=there, device_id_type=MESH)
         return carry
 
-    for k in range(1, 16):
-        there = (row, (col + k) % 16)
-        pl.semaphore_signal(barrier, inc=1, device_id=there, device_id_type=MESH)
-    lax.fori_loop(1, 8, greet, 0)
+    lax.fori_loop(4, 8, greet, 0)
+    lax.fori_loop(1, 4, greet, 0)
+    for k in around:
+        if k:
+            there = (row, lax.rem(col + k, 16))
+            pl.semaphore_signal(barrier, inc=1, device_id=there, device_id_type=MESH)
 
     in_slots.wait()
     iota32 = lax.broadcasted_iota(jnp.int32, (32, 128), 0)

time: 70.3 us -> 71.9 us (1.023); the launches traced: 68.9 us -> 71.5 us
  Pallas kernels: 66.2 us -> 68.7 us
    pallas_call x1, Pallas kernels: 66.2 us -> 68.7 us  [per_device(): pl.pallas_call(kernel, out_shape=(jax.ShapeDtypeStruct((PAR_DEV, BANDS),...]
where the time goes in v2:
time: 71.9 us; the launch traced here: 71.5 us
  Pallas kernels  68.7 us (96%)
  local copies, waits for them, and re-layouts  2.11 us (3%)
    pallas_call x1, Pallas kernels, per_device(): pl.pallas_call(kernel, out_shape=(jax.ShapeDtypeStruct((PAR_DEV, BANDS),...  68.7 us
    unnamed x2, local copies, waits for them, and re-layouts  2.11 us

profile of v2, /device:TPU:1, one launch (start us, length us, event | category | flops | bytes accessed | tf_op | source)
XLA Modules:
  0.0 71.5 jit_solution(3556061490419125954)
XLA Ops:
  0.6 68.7 %shard_map.50 = (f32[1024,128]{1,0:T(8,128)S(1)}, f32[4096,128]{1,0:T(8,128)S(1)}) custom-call(f32[4096,128]{1,0:T(8,128)} %bitcast.4, s32[32,128]{1,0:T(8,128)} %slots.1, s32[32,128]{1,0:T(8,128)} %bitcast.5), custom_call_target="tpu_custom_call" | custom-call | tf_op jit(solution)/shard_map/pallas_call | solution.py:305
  69.4 0.8 %copy.7 = f32[1024,128]{1,0:T(8,128)} copy(f32[1024,128]{1,0:T(8,128)S(1)} %get-tuple-element.8) | data formatting | bytes 1048576
  70.2 1.3 %copy.8 = f32[32,128,128]{2,1,0:T(8,128)} copy(f32[32,128,128]{2,1,0:T(8,128)S(1)} %bitcast.3) | data formatting | bytes 4194304

commit v3 on v2

--- a/solution.py
+++ b/solution.py
@@ -1,4 +1,5 @@
 import itertools
+import random
 
 import jax
 import jax.numpy as jnp
@@ -24,8 +25,9 @@
 I16 = jnp.int16
 
 
-SHIFTS = list(itertools.product(range(4), repeat=2))
-ORDER = [(t, (t + u) % 4, (t + v) % 4) for u, v in SHIFTS[1:] + SHIFTS[:1] for t in (2, 1, 3, 0)]
+ORDER = [d for d in itertools.product(range(4), repeat=3) if any(d)]
+random.Random(0).shuffle(ORDER)
+ORDER.append((0, 0, 0))
 CODES = [d[0] + 4 * d[1] + 16 * d[2] for d in ORDER]
 
 
@@ -51,9 +53,39 @@
     return jnp.concatenate([v] * 16, axis=0)
 
 
+def subtract(out, acc, colb, ids, block, done=lambda n: None):
+    r2 = jnp.concatenate(split(block), axis=1)
+    rows = [over_rows(v) for v in ids]
+    for n in range(16):
+        part = slice(n * 256, n * 256 + 256)
+        px = colb[part, :].astype(I16)
+        table = jnp.concatenate([onehot(px == v) for v in rows], axis=1)
+        s = jnp.dot(table, r2, preferred_element_type=F32)
+        out[part, :] = acc[part, :] - s[:, :128] - s[:, 128:]
+        done(n)
+
+
+def finish(tot, acc, colb, ids, last, means_out, anom_out, res, sems):
+    means = pltpu.make_async_copy(tot, means_out, sems.at[4])
+    means.start()
+    copies = []
+
+    def done(n):
+        if n % 4 == 3:
+            part = pl.ds((n // 4) * 1024, 1024)
+            copy = pltpu.make_async_copy(res.at[part], anom_out.at[part], sems.at[n // 4])
+            copy.start()
+            copies.append(copy)
+
+    subtract(res, acc, colb, [ids[h : h + 1, :] for h in range(2)], last[...], done)
+    for copy in copies:
+        copy.wait()
+    means.wait()
+
+
 def kernel(
-    raster, slots, targets, tot, acc,
-    x2, b1, colb, tcol, num, m2,
+    raster, slots, targets, tot, acc, colb, ids_out, last_out,
+    x2, b1, tcol, num, m2,
     send, got, rep, ret, small, slot_v, targ_v,
     s_in, s_send, s_got, s_ret,
 ):
@@ -268,14 +300,7 @@
 
     lane1 = lax.broadcasted_iota(jnp.int32, (1, 128), 1)
 
-    def subtract(n, r2, ids):
-        part = pl.ds(pl.multiple_of(n * 256, 256), 256)
-        px = colb[part, :].astype(I16)
-        table = jnp.concatenate([onehot(px == v) for v in ids], axis=1)
-        s = jnp.dot(table, r2, preferred_element_type=F32)
-        acc[part, :] = acc[part, :] - s[:, :128] - s[:, 128:]
-
-    def read_batch(b, carry):
+    def fetch(b):
         here = pl.ds(pl.multiple_of(b * ROWS, ROWS), ROWS)
         g, bb = lax.div(b, 8), lax.rem(b, 8)
         ids = []
@@ -284,14 +309,20 @@
             for m in range(4):
                 base = lin(*place(pick(CODES[4 * h + m :: 8], bb), 1), g) * CAP
                 v = v + jnp.where(lane1 // 32 == m, base, 0)
-            ids.append(over_rows(v))
+            ids.append(v)
         wait_bytes(ret.at[here], s_ret.at[b])
-        r2 = jnp.concatenate(split(ret[here, :]), axis=1)
-        for n in range(16):
-            subtract(n, r2, ids)
-        return carry
-
-    lax.fori_loop(0, BATCHES, read_batch, 0)
+        return ids, ret[here, :]
+
+    def read_batch(b, carry):
+        ids, block = fetch(b)
+        subtract(acc, acc, colb, ids, block)
+        return carry
+
+    lax.fori_loop(0, BATCHES - 1, read_batch, 0)
+    ids, block = fetch(jnp.int32(BATCHES - 1))
+    for h in range(2):
+        ids_out[h : h + 1, :] = ids[h]
+    last_out[...] = block
 
     wait_bytes(send.at[pl.ds(0, (DEVS - 1) * MSG)], s_send.at[0])
     wait_bytes(rep.at[pl.ds(0, (DEVS - 1) * CAP)], s_send.at[1])
@@ -302,18 +333,20 @@
     here = pl.BlockSpec(memory_space=pltpu.VMEM)
     outside = pl.BlockSpec(memory_space=pltpu.HBM)
     table = pltpu.VMEM((PIX, BANDS), F32)
-    means, anomaly = pl.pallas_call(
+    partial = pl.pallas_call(
         kernel,
         out_shape=(
             jax.ShapeDtypeStruct((PAR_DEV, BANDS), F32),
             jax.ShapeDtypeStruct((PIX, BANDS), F32),
+            jax.ShapeDtypeStruct((PIX, 128), jnp.int32),
+            jax.ShapeDtypeStruct((8, 128), jnp.int32),
+            jax.ShapeDtypeStruct((ROWS, BANDS), F32),
         ),
         in_specs=[outside] * 3,
-        out_specs=(here, here),
+        out_specs=(here,) * 5,
         scratch_shapes=[
             pltpu.VMEM((PIX, 2 * BANDS), BF),
             pltpu.VMEM((PIX, 128), BF),
-            pltpu.VMEM((PIX, 128), jnp.int32),
             pltpu.VMEM((PIX, 128), jnp.int32),
             pltpu.VMEM((PAR_DEV, BANDS), F32),
             pltpu.VMEM((PAR_DEV, 2 * BANDS), BF),
@@ -333,6 +366,17 @@
             collective_id=0, has_side_effects=True, vmem_limit_bytes=48 * 2**20
         ),
     )(*(pltpu.with_memory_space_constraint(v, pltpu.HBM) for v in operands))
+    means, anomaly = pl.pallas_call(
+        finish,
+        out_shape=(
+            jax.ShapeDtypeStruct((PAR_DEV, BANDS), F32),
+            jax.ShapeDtypeStruct((PIX, BANDS), F32),
+        ),
+        in_specs=[here] * 5,
+        out_specs=(outside, outside),
+        scratch_shapes=[table, pltpu.SemaphoreType.DMA((5,))],
+        compiler_params=pltpu.CompilerParams(vmem_limit_bytes=16 * 2**20),
+    )(*partial)
     return means, anomaly.reshape(raster.shape)
 
 

time: 71.9 us -> 72.6 us (level)
  Pallas kernels: 68.7 us -> 71.8 us
  local copies, waits for them, and re-layouts: 2.11 us -> 0 us
    unnamed x2 -> x0, local copies, waits for them, and re-layouts: 2.11 us -> none
    pallas_call x0 -> x1, Pallas kernels: none -> 1.67 us  [per_device(): pl.pallas_call(finish, out_shape=(jax.ShapeDtypeStruct((PAR_DEV, BANDS),...]
    pallas_call x1, Pallas kernels: 68.7 us -> 70.1 us  [per_device(): pl.pallas_call(kernel, out_shape=(jax.ShapeDtypeStruct((PAR_DEV, BANDS),...]
where the time goes in v3:
time: 72.6 us; the launch traced here: 72.4 us
  Pallas kernels  71.8 us (99%)
    pallas_call x1, Pallas kernels, per_device(): pl.pallas_call(kernel, out_shape=(jax.ShapeDtypeStruct((PAR_DEV, BANDS),...  70.1 us
    pallas_call x1, Pallas kernels, per_device(): pl.pallas_call(finish, out_shape=(jax.ShapeDtypeStruct((PAR_DEV, BANDS),...  1.67 us

profile of v3, /device:TPU:1, one launch (start us, length us, event | category | flops | bytes accessed | tf_op | source)
XLA Modules:
  0.0 72.4 jit_solution(1083178849577709125)
XLA Ops:
  0.6 70.1 %shard_map.50 = (f32[1024,128]{1,0:T(8,128)S(1)}, f32[4096,128]{1,0:T(8,128)S(1)}, s32[4096,128]{1,0:T(8,128)S(1)}, s32[8,128]{1,0:T(8,128)S(1)}, f32[256,128]{1,0:T(8,128)S(1)}) custom-call(f32[4096,128]{1,0:T(8,128)} %bitcast.3, s32[32,128]{1,0:T(8,128)} %slots.1, s32[32,128]{1,0:T(8,128)} %bitcast.4), custom_call_target="tpu_custom_call" | custom-call | tf_op jit(solution)/shard_map/pallas_call | solution.py:336
  70.8 1.7 %shard_map.51 = (f32[1024,128]{1,0:T(8,128)}, f32[4096,128]{1,0:T(8,128)}) custom-call(f32[1024,128]{1,0:T(8,128)S(1)} %get-tuple-element.9.tot, f32[4096,128]{1,0:T(8,128)S(1)} %get-tuple-element.10.acc, s32[4096,128]{1,0:T(8,128)S(1)} %get-tuple-element.11.colb, s32[8,128]{1,0:T(8,128)S(1)} %get-tuple-element.12.ids, f32[256,128]{1,0:T(8,128)S(1)} %get-tuple-element.13.last), custom_call_target="tpu_custom_call" | custom-call | tf_op jit(solution)/shard_map/pallas_call | solution.py:369

commit v4 on v3

--- a/solution.py
+++ b/solution.py
@@ -1,5 +1,4 @@
 import itertools
-import random
 
 import jax
 import jax.numpy as jnp
@@ -25,9 +24,8 @@
 I16 = jnp.int16
 
 
-ORDER = [d for d in itertools.product(range(4), repeat=3) if any(d)]
-random.Random(0).shuffle(ORDER)
-ORDER.append((0, 0, 0))
+SHIFTS = list(itertools.product(range(4), repeat=2))
+ORDER = [(t, (t + u) % 4, (t + v) % 4) for u, v in SHIFTS[1:] + SHIFTS[:1] for t in (2, 1, 3, 0)]
 CODES = [d[0] + 4 * d[1] + 16 * d[2] for d in ORDER]
 
 
@@ -136,21 +134,17 @@
         in_raster[-1].start()
     barrier = pltpu.get_barrier_semaphore()
 
-    around = [(k + 10) % 16 for k in range(16)]
-
     def greet(n, carry):
-        far = lax.rem(row + n, 8)
-        for k in around:
-            there = (far, lax.rem(col + k, 16))
+        far = (row + n) % 8
+        for k in range(16):
+            there = (far, (col + k) % 16)
             pl.semaphore_signal(barrier, inc=1, device_id=there, device_id_type=MESH)
         return carry
 
-    lax.fori_loop(4, 8, greet, 0)
-    lax.fori_loop(1, 4, greet, 0)
-    for k in around:
-        if k:
-            there = (row, lax.rem(col + k, 16))
-            pl.semaphore_signal(barrier, inc=1, device_id=there, device_id_type=MESH)
+    for k in range(1, 16):
+        there = (row, (col + k) % 16)
+        pl.semaphore_signal(barrier, inc=1, device_id=there, device_id_type=MESH)
+    lax.fori_loop(1, 8, greet, 0)
 
     in_slots.wait()
     iota32 = lax.broadcasted_iota(jnp.int32, (32, 128), 0)

time: 72.6 us -> 72.7 us (level)
  the two profiles are of different devices: /device:TPU:1 before, /device:TPU:105 now
where the time goes in v4:
time: 72.7 us; the launch traced here: 72.6 us
  Pallas kernels  71.9 us (99%)
    pallas_call x1, Pallas kernels, per_device(): pl.pallas_call(kernel, out_shape=(jax.ShapeDtypeStruct((PAR_DEV, BANDS),...  70.3 us
    pallas_call x1, Pallas kernels, per_device(): pl.pallas_call(finish, out_shape=(jax.ShapeDtypeStruct((PAR_DEV, BANDS),...  1.67 us

profile of v4, /device:TPU:105, one launch (start us, length us, event | category | flops | bytes accessed | tf_op | source)
XLA Modules:
  0.0 72.6 jit_solution(4839858222316225492)
XLA Ops:
  0.6 70.3 %shard_map.50 = (f32[1024,128]{1,0:T(8,128)S(1)}, f32[4096,128]{1,0:T(8,128)S(1)}, s32[4096,128]{1,0:T(8,128)S(1)}, s32[8,128]{1,0:T(8,128)S(1)}, f32[256,128]{1,0:T(8,128)S(1)}) custom-call(f32[4096,128]{1,0:T(8,128)} %bitcast.3, s32[32,128]{1,0:T(8,128)} %slots.1, s32[32,128]{1,0:T(8,128)} %bitcast.4), custom_call_target="tpu_custom_call" | custom-call | tf_op jit(solution)/shard_map/pallas_call | solution.py:330
  70.9 1.7 %shard_map.51 = (f32[1024,128]{1,0:T(8,128)}, f32[4096,128]{1,0:T(8,128)}) custom-call(f32[1024,128]{1,0:T(8,128)S(1)} %get-tuple-element.9.tot, f32[4096,128]{1,0:T(8,128)S(1)} %get-tuple-element.10.acc, s32[4096,128]{1,0:T(8,128)S(1)} %get-tuple-element.11.colb, s32[8,128]{1,0:T(8,128)S(1)} %get-tuple-element.12.ids, f32[256,128]{1,0:T(8,128)S(1)} %get-tuple-element.13.last), custom_call_target="tpu_custom_call" | custom-call | tf_op jit(solution)/shard_map/pallas_call | solution.py:363

commit v5 on v1

--- a/solution.py
+++ b/solution.py
@@ -19,7 +19,7 @@
 BLK = 8
 ROWS = BLK * CAP
 BATCHES = DEVS // BLK
-EARLY = 2
+EARLY = 1
 BF = jnp.bfloat16
 F32 = jnp.float32
 I16 = jnp.int16

time: 70.3 us -> 73.2 us (1.041); the launches traced: 68.9 us -> 73.1 us
  Pallas kernels: 66.2 us -> 70.3 us
    pallas_call x1, Pallas kernels: 66.2 us -> 70.3 us  [per_device(): pl.pallas_call(kernel, out_shape=(jax.ShapeDtypeStruct((PAR_DEV, BANDS),...]
where the time goes in v5:
time: 73.2 us; the launch traced here: 73.1 us
  Pallas kernels  70.3 us (96%)
  local copies, waits for them, and re-layouts  2.11 us (3%)
    pallas_call x1, Pallas kernels, per_device(): pl.pallas_call(kernel, out_shape=(jax.ShapeDtypeStruct((PAR_DEV, BANDS),...  70.3 us
    unnamed x2, local copies, waits for them, and re-layouts  2.11 us

profile of v5, /device:TPU:1, one launch (start us, length us, event | category | flops | bytes accessed | tf_op | source)
XLA Modules:
  0.0 73.1 jit_solution(1401811415804689885)
XLA Ops:
  0.6 70.3 %shard_map.50 = (f32[1024,128]{1,0:T(8,128)S(1)}, f32[4096,128]{1,0:T(8,128)S(1)}) custom-call(f32[4096,128]{1,0:T(8,128)} %bitcast.4, s32[32,128]{1,0:T(8,128)} %slots.1, s32[32,128]{1,0:T(8,128)} %bitcast.5), custom_call_target="tpu_custom_call" | custom-call | tf_op jit(solution)/shard_map/pallas_call | solution.py:303
  70.9 0.8 %copy.7 = f32[1024,128]{1,0:T(8,128)} copy(f32[1024,128]{1,0:T(8,128)S(1)} %get-tuple-element.8) | data formatting | bytes 1048576
  71.7 1.3 %copy.8 = f32[32,128,128]{2,1,0:T(8,128)} copy(f32[32,128,128]{2,1,0:T(8,128)S(1)} %bitcast.3) | data formatting | bytes 4194304
